TPU v7x, 32 devices: a whole 2x2x4 slice. The times are simulated.
32 devices in a mesh: plant: 2 (over x), section: 16 (over z, y, core).
Axes of the slice: x: 2, y: 2, z: 4, core: 2. Of those that a mesh axis runs over, the one named last changes fastest.
Arguments:
- dynamics_operator: bfloat16 [1024, 512], P('plant'), parts along dimension 0
- control_gain_array: bfloat16 [1024, 256], P('plant'), parts along dimension 0
- kkt_inverse: bfloat16 [1536, 768], P('plant'), parts along dimension 0
- lin_state: float32 [1024, 4096], P(('plant', 'section')), parts along dimension 0, may hold values from -6 to 6
- lin_input: float32 [512, 4096], P(('plant', 'section')), parts along dimension 0, may hold values from -6 to 6
- block_start: int32 [2], P('plant'), parts along dimension 0, may hold values from 0 to 15
- period: int32 [2], P('plant'), parts along dimension 0, may hold values from 2048 to 4096
Outputs:
- state_traj: float32 [1024, 4096], P('plant', 'section'), parts along dimension 0
- input_traj: float32 [512, 4096], P('plant', 'section'), parts along dimension 0
- consensus: float32 [1024, 4096], P('plant', 'section'), parts along dimension 0
- residual_norms: float32 [4], P('plant'), parts along dimension 0
There are 2 independent parts, one for each index of `plant`. A program takes and returns all parts, laid end to end along the dimension named above; each array names one. Nothing has to cross between parts.
Inputs may be any that keep to these rules, and one draw needn't show every extreme that they name: Device d of the section axis holds the block of logical sections starting at 256 * ((d - block_start) mod the axis's size).
All inputs are finite; a program needn't handle non-finite values.
Results may differ from a plain program's by a relative error of at most 0.0045.
Values sent between devices are 32-bit elements; how exact they have to be, the bound alone decides.
A program may use at most 64 MiB of HBM per device.

v0:
```python
import jax
import jax.numpy as jnp
from jax import lax
from jax.sharding import PartitionSpec as P

ITERS = 4


RHO = 1.0


def padded(cells, sides, width):
    for axis, dim in sides:
        count = lax.axis_size(axis)
        head = lax.slice_in_dim(cells, 0, width, axis=dim)
        tail = lax.slice_in_dim(cells, cells.shape[dim] - width, cells.shape[dim], axis=dim)
        cells = jnp.concatenate(
            [
                lax.ppermute(tail, axis, [(i, (i + 1) % count) for i in range(count)]),
                cells,
                lax.ppermute(head, axis, [((i + 1) % count, i) for i in range(count)]),
            ],
            axis=dim,
        )
    return cells


def adjoint(dynamics_operator, control_gain_array, target):
    rounded = target.astype(jnp.bfloat16)
    contract = (((0,), (0,)), ((), ()))
    upper_part = lax.dot_general(
        dynamics_operator, rounded, contract, preferred_element_type=jnp.float32
    )
    lower_part = lax.dot_general(
        control_gain_array, rounded, contract, preferred_element_type=jnp.float32
    )
    return jnp.concatenate([upper_part, lower_part], axis=0)


def estimate_condition(dynamics_operator, control_gain_array, merged_pieces, condition_lines):
    rounded = merged_pieces.astype(jnp.bfloat16)
    return jnp.dot(
        dynamics_operator, rounded[:condition_lines], preferred_element_type=jnp.float32
    ) + jnp.dot(control_gain_array, rounded[condition_lines:], preferred_element_type=jnp.float32)


def pick_column(values, selector):
    return jnp.sum(jnp.where(selector, values, 0.0), axis=1, keepdims=True)


def local(
    dynamics_operator, control_gain_array, kkt_inverse, lin_state, lin_input, block_start, period
):
    condition_lines = dynamics_operator.shape[0]
    cycle_size = lax.axis_size("section")
    block_width = lin_state.shape[1] // cycle_size
    block_index = (lax.axis_index("section") - block_start[0]) % cycle_size
    section_ids = block_index * block_width + jnp.arange(block_width, dtype=jnp.int32)
    working_segment = (section_ids < period[0])[None, :]
    is_first = (section_ids == 0)[None, :]
    is_last = (section_ids == period[0] - 1)[None, :]
    state_parts = lin_state.reshape(lin_state.shape[0], cycle_size, block_width)
    input_parts = lin_input.reshape(lin_input.shape[0], cycle_size, block_width)
    cost_state = lax.all_to_all(state_parts, "section", split_axis=1, concat_axis=0, tiled=True)
    cost_input = lax.all_to_all(input_parts, "section", split_axis=1, concat_axis=0, tiled=True)
    neg_part = -jnp.concatenate([cost_state[:, 0, :], cost_input[:, 0, :]], axis=0)
    product = jnp.dot(
        kkt_inverse, neg_part.astype(jnp.bfloat16), preferred_element_type=jnp.float32
    )
    neg_cost, product = (neg_part, product)
    zero_block = jnp.zeros((condition_lines, block_width), jnp.float32)
    input_zero = jnp.zeros((neg_cost.shape[0] - condition_lines, block_width), jnp.float32)
    consensus = zero_block
    dual_state = zero_block
    multiplier_link = zero_block
    ahead_z = zero_block
    merged_pieces = jnp.zeros_like(neg_cost)
    primal_part = jnp.float32(0.0)
    dual_part = jnp.float32(0.0)
    for iteration in range(ITERS):
        if iteration > 0:
            right_side = (
                neg_cost
                + RHO * jnp.concatenate([consensus - dual_state, input_zero], axis=0)
                + RHO * adjoint(dynamics_operator, control_gain_array, ahead_z - multiplier_link)
            )
            product = jnp.dot(
                kkt_inverse, right_side.astype(jnp.bfloat16), preferred_element_type=jnp.float32
            )
        merged_pieces = jnp.where(working_segment, product, 0.0)
        expected_condition = estimate_condition(
            dynamics_operator, control_gain_array, merged_pieces, condition_lines
        )
        own_sum = merged_pieces[:condition_lines] + dual_state
        passed_quantity = expected_condition + multiplier_link
        stacked = jnp.concatenate([passed_quantity, own_sum], axis=0)
        edges = jnp.concatenate([stacked[:, :1], stacked[:, -1:]], axis=1)
        rim_cols = padded(edges, (("section", 1),), 1)
        closing_carried, closing_own = lax.psum(
            (pick_column(passed_quantity, is_last), pick_column(own_sum, is_first)), "section"
        )
        previous = jnp.concatenate(
            [rim_cols[:condition_lines, 0:1], passed_quantity[:, :-1]], axis=1
        )
        previous = jnp.where(is_first, closing_carried, previous)
        newest_agreement = jnp.where(working_segment, 0.5 * (own_sum + previous), 0.0)
        ahead_tail = 0.5 * (rim_cols[condition_lines:, -1:] + passed_quantity[:, -1:])
        onward_refreshed = jnp.concatenate([newest_agreement[:, 1:], ahead_tail], axis=1)
        onward_refreshed = jnp.where(
            is_last, 0.5 * (closing_own + closing_carried), onward_refreshed
        )
        change_z = newest_agreement - consensus
        dual_state = jnp.where(
            working_segment, dual_state + merged_pieces[:condition_lines] - newest_agreement, 0.0
        )
        multiplier_link = jnp.where(
            working_segment, multiplier_link + expected_condition - onward_refreshed, 0.0
        )
        if iteration == ITERS - 1:
            primal_part = jnp.sum(
                jnp.where(
                    working_segment,
                    (merged_pieces[:condition_lines] - newest_agreement) ** 2
                    + (expected_condition - onward_refreshed) ** 2,
                    0.0,
                )
            )
            dual_part = RHO * RHO * jnp.sum(change_z * change_z)
        consensus = newest_agreement
        ahead_z = onward_refreshed
    primal_total, dual_total = lax.psum((primal_part, dual_part), "section")
    residual_norms = jnp.stack([jnp.sqrt(primal_total), jnp.sqrt(dual_total)])
    return (
        merged_pieces[:condition_lines],
        merged_pieces[condition_lines:],
        consensus,
        residual_norms,
    )


def solution(mesh):
    return jax.shard_map(
        local,
        mesh=mesh,
        in_specs=(
            P("plant", None),
            P("plant", None),
            P("plant", None),
            P(("plant", "section"), None),
            P(("plant", "section"), None),
            P("plant"),
            P("plant"),
        ),
        out_specs=(P("plant", "section"), P("plant", "section"), P("plant", "section"), P("plant")),
        check_vma=False,
    )
```

profile of v0, /device:TPU:0, one launch (start us, length us, event | category | flops | bytes accessed | tf_op | source)
XLA Modules:
  0.0 239.6 jit_solution(15876004732450806307)
XLA Ops:
  0.7 1.8 copy.49
  2.5 7.4 %all-to-all-start.1 = ((f32[16,16,256]{2,0,1:T(8,128)}), f32[16,16,256]{2,0,1:T(8,128)S(1)}, u32[]{:S(2)}, u32[]{:S(2)}) async-start(f32[16,16,256]{2,0,1:T(8,128)} %bitcast.93), calls=%async_computation.1 | async-start | bytes 524288 | tf_op jit(solution)/shard_map/all_to_all | solution.py:65
  9.9 0.9 copy.48
  10.7 9.2 %all-to-all-done.1 = f32[16,16,256]{2,0,1:T(8,128)S(1)} async-done(((f32[16,16,256]{2,0,1:T(8,128)}), f32[16,16,256]{2,0,1:T(8,128)S(1)}, u32[]{:S(2)}, u32[]{:S(2)}) %all-to-all-start.1) | async-done | bytes 262176 | tf_op jit(solution)/shard_map/all_to_all | solution.py:65
  19.9 3.6 %all-to-all-start = ((f32[32,16,256]{2,0,1:T(8,128)}), f32[32,16,256]{2,0,1:T(8,128)S(1)}, u32[]{:S(2)}, u32[]{:S(2)}) async-start(f32[32,16,256]{2,0,1:T(8,128)} %bitcast.92), calls=%async_computation | async-start | bytes 1048576 | tf_op jit(solution)/shard_map/all_to_all | solution.py:64
  24.8 0.1 copy.34
  25.0 12.7 %all-to-all-done = f32[32,16,256]{2,0,1:T(8,128)S(1)} async-done(((f32[32,16,256]{2,0,1:T(8,128)}), f32[32,16,256]{2,0,1:T(8,128)S(1)}, u32[]{:S(2)}, u32[]{:S(2)}) %all-to-all-start) | async-done | bytes 524320 | tf_op jit(solution)/shard_map/all_to_all | solution.py:64
  37.7 0.2 copy.33
  37.9 0.5 fusion.70
  38.5 0.5 copy-done.1
  39.0 0.3 fusion.45
  39.4 0.5 copy-done.2
  39.9 0.3 select_reduce_fusion.7
  40.2 0.2 collective-permute-start
  40.4 4.3 %collective-permute-start.1 = (f32[1024,1]{0,1:T(1,128)S(1)}, f32[1024,1]{0,1:T(1,128)S(1)}, u32[]{:S(2)}, u32[]{:S(2)}) collective-permute-start(f32[1024,1]{0,1:T(1,128)S(1)} %get-tuple-element.53), channel_id=1, source_target_pairs={{1,0},{2,1},{3,2},{4,3},{5,4},{6,5},{7,6},{8,7},{9,8},{10,9},{11,1... | collective-permute-start | bytes 12296 | tf_op jit(solution)/shard_map/ppermute | solution.py:21
  44.7 29.5 %all-reduce.7 = (f32[512,1]{0,1:T(1,128)S(1)}, f32[512,1]{0,1:T(1,128)S(1)}) all-reduce(f32[512,1]{0,1:T(1,128)S(1)} %bitcast.121, f32[512,1]{0,1:T(1,128)S(1)} %bitcast.120), channel_id=1, replica_groups=mesh['plant'=2,'section'=16] {'section'}, use_global_device_ids=true, to_apply=%region_1.2 | all-reduce | flops 1024 | bytes 8192 | tf_op jit(solution)/shard_map/psum | solution.py:99
  74.2 1.3 fusion.30
  75.6 0.2 subtract_convert_fusion.2
  75.8 0.2 convolution_bitcast_fusion.5
  76.0 0.3 convolution_bitcast_fusion.2
  76.3 0.6 fusion.71
  76.9 0.6 copy-done.8
  77.4 0.2 select_reduce_fusion.4
  77.6 0.3 fusion.43
  78.0 0.9 select_reduce_fusion.5
  78.9 4.4 %collective-permute-start.3 = (f32[1024,1]{0,1:T(1,128)S(1)}, f32[1024,1]{0,1:T(1,128)S(1)}, u32[]{:S(2)}, u32[]{:S(2)}) collective-permute-start(f32[1024,1]{0,1:T(1,128)S(1)} %get-tuple-element.51), channel_id=1, source_target_pairs={{1,0},{2,1},{3,2},{4,3},{5,4},{6,5},{7,6},{8,7},{9,8},{10,9},{11,1... | collective-permute-start | bytes 12296 | tf_op jit(solution)/shard_map/ppermute | solution.py:21
  83.4 29.6 %all-reduce.6 = (f32[512,1]{0,1:T(1,128)S(1)}, f32[512,1]{0,1:T(1,128)S(1)}) all-reduce(f32[512,1]{0,1:T(1,128)} %bitcast.126, f32[512,1]{0,1:T(1,128)S(1)} %bitcast.116), channel_id=1, replica_groups=mesh['plant'=2,'section'=16] {'section'}, use_global_device_ids=true, to_apply=%region_5.6 | all-reduce | flops 1024 | bytes 8192 | tf_op jit(solution)/shard_map/psum | solution.py:99
  113.0 1.3 fusion.31
  114.3 0.2 subtract_convert_fusion.1
  114.6 0.2 convolution_bitcast_fusion.4
  114.8 0.3 convolution_bitcast_fusion.1
  115.1 0.4 copy-done.10
  115.5 0.6 fusion.72
  116.1 0.5 copy-done.6
  116.5 0.2 select_reduce_fusion.2
  116.7 0.3 fusion.41
  117.1 0.9 select_reduce_fusion.3
  118.0 0.6 pad_maximum_fusion.3
  118.6 4.4 %collective-permute-start.5 = (f32[1024,1]{0,1:T(1,128)}, f32[1024,1]{0,1:T(1,128)}, u32[]{:S(2)}, u32[]{:S(2)}) collective-permute-start(f32[1024,1]{0,1:T(1,128)} %get-tuple-element.49), channel_id=1, source_target_pairs={{1,0},{2,1},{3,2},{4,3},{5,4},{6,5},{7,6},{8,7},{9,8},{10,9},{11,1... | collective-permute-start | bytes 12296 | tf_op jit(solution)/shard_map/ppermute | solution.py:21
  123.0 29.6 %all-reduce.5 = (f32[512,1]{0,1:T(1,128)S(1)}, f32[512,1]{0,1:T(1,128)S(1)}) all-reduce(f32[512,1]{0,1:T(1,128)} %bitcast.127, f32[512,1]{0,1:T(1,128)S(1)} %bitcast.117), channel_id=1, replica_groups=mesh['plant'=2,'section'=16] {'section'}, use_global_device_ids=true, to_apply=%region_9.10 | all-reduce | flops 1024 | bytes 8192 | tf_op jit(solution)/shard_map/psum | solution.py:99
  152.6 0.6 copy-done.22
  153.2 1.3 fusion.33
  154.5 0.7 fusion.52
  155.2 0.2 subtract_convert_fusion
  155.4 0.2 convolution_bitcast_fusion.3
  155.7 0.3 convolution_bitcast_fusion
  156.0 0.4 copy-done.11
  156.4 1.3 fusion.73
  157.7 0.9 copy-done.12
  158.6 0.7 slice.194
  159.3 1.8 copy.39
  161.1 1.4 fusion.39
  162.5 2.6 %select_reduce_fusion.1 = (f32[512]{0:T(512)}, f32[512,256]{0,1:T(8,128)S(1)}, f32[512]{0:T(512)}, f32[512,256]{0,1:T(8,128)S(1)}, f32[512,256]{0,1:T(8,128)}) fusion(pred[256]{0:T(512)(128)(4,1)S(1)} %get-tuple-element.74, f32[512,256]{0,1:T(8,128)S(1)} %get-tuple-element.70, f32[512,1]{0,1:T(1,128)} %copy-done.21, f32[512,255]{0,1:T(8,128)S(1)} %copy-done.17, ...), kind=kOutput, calls=%fused_computation.61 | convolution fusion | flops 68811776 | bytes 5118720 | tf_op jit(solution)/shard_map/dot_general | solution.py:44
  165.1 0.8 copy-done.18
  165.9 0.6 pad_maximum_fusion
  166.5 0.5 collective-permute-start.6
  167.0 33.5 %all-reduce.4 = (f32[512,1]{0,1:T(1,128)S(1)}, f32[512,1]{0,1:T(1,128)S(1)}) all-reduce(f32[512,1]{0,1:T(1,128)} %bitcast.118, f32[512,1]{0,1:T(1,128)} %bitcast.119), channel_id=1, replica_groups=mesh['plant'=2,'section'=16] {'section'}, use_global_device_ids=true, to_apply=%region_13.14 | all-reduce | flops 1024 | bytes 8192 | tf_op jit(solution)/shard_map/psum | solution.py:99
  200.6 1.4 fusion.24
  202.0 1.0 copy.40
  203.0 0.7 fusion.51
  203.8 1.7 fusion.29
  205.5 2.0 copy.38
  207.5 30.2 %all-reduce.3 = (f32[]{:T(128)}, f32[]{:T(128)}) all-reduce(f32[]{:T(128)} %get-tuple-element.21, f32[]{:T(128)} %get-tuple-element.20), channel_id=1, replica_groups=mesh['plant'=2,'section'=16] {'section'}, use_global_device_ids=true, to_apply=%region_19.20 | all-reduce | flops 2 | bytes 16 | tf_op jit(solution)/shard_map/psum | solution.py:131
  239.1 0.6 pad_maximum_fusion.8
  (67 shorter events, 0.6 us)
Async XLA Ops:
  0.6 37.3 %copy-start = (bf16[768,768]{1,0:T(8,128)(2,1)S(1)}, bf16[768,768]{1,0:T(8,128)(2,1)}, u32[]{:S(2)}) copy-start(bf16[768,768]{1,0:T(8,128)(2,1)} %param.9) | copy-start | bytes 3538948
  0.6 9.2 %copy-start.20 = (f32[32,4096]{1,0:T(8,128)S(1)}, f32[32,4096]{1,0:T(8,128)}, u32[]{:S(2)}) copy-start(f32[32,4096]{1,0:T(8,128)} %param.10) | copy-start | bytes 1572868
  2.5 17.4 %all-to-all-start.1 = ((f32[16,16,256]{2,0,1:T(8,128)}), f32[16,16,256]{2,0,1:T(8,128)S(1)}, u32[]{:S(2)}, u32[]{:S(2)}) async-start(f32[16,16,256]{2,0,1:T(8,128)} %bitcast.93), calls=%async_computation.1 | async-start | bytes 524288 | tf_op jit(solution)/shard_map/all_to_all | solution.py:65
  19.9 17.8 %all-to-all-start = ((f32[32,16,256]{2,0,1:T(8,128)}), f32[32,16,256]{2,0,1:T(8,128)S(1)}, u32[]{:S(2)}, u32[]{:S(2)}) async-start(f32[32,16,256]{2,0,1:T(8,128)} %bitcast.92), calls=%async_computation | async-start | bytes 1048576 | tf_op jit(solution)/shard_map/all_to_all | solution.py:64
  25.0 51.3 %copy-start.9 = (f32[256,256]{0,1:T(8,128)}, f32[256,256]{0,1:T(8,128)S(1)}, u32[]{:S(2)}) copy-start(f32[256,256]{0,1:T(8,128)S(1)} %copy.34) | copy-start | bytes 786436
  37.9 1.0 copy-start.1
  38.5 1.0 copy-start.7
  39.0 0.9 copy-start.2
  40.2 34.0 %collective-permute-start = (f32[1024,1]{0,1:T(1,128)S(1)}, f32[1024,1]{0,1:T(1,128)S(1)}, u32[]{:S(2)}, u32[]{:S(2)}) collective-permute-start(f32[1024,1]{0,1:T(1,128)S(1)} %get-tuple-element.52), channel_id=1, source_target_pairs={{0,1},{1,2},{2,3},{3,4},{4,5},{5,6},{6,7},{7,8},{8,9},{9,10},{10,1... | collective-permute-start | bytes 12296 | tf_op jit(solution)/shard_map/ppermute | solution.py:19
  40.4 35.1 %collective-permute-start.1 = (f32[1024,1]{0,1:T(1,128)S(1)}, f32[1024,1]{0,1:T(1,128)S(1)}, u32[]{:S(2)}, u32[]{:S(2)}) collective-permute-start(f32[1024,1]{0,1:T(1,128)S(1)} %get-tuple-element.53), channel_id=1, source_target_pairs={{1,0},{2,1},{3,2},{4,3},{5,4},{6,5},{7,6},{8,7},{9,8},{10,9},{11,1... | collective-permute-start | bytes 12296 | tf_op jit(solution)/shard_map/ppermute | solution.py:21
  76.3 1.1 copy-start.8
  77.6 1.2 copy-start.5
  78.9 34.1 %collective-permute-start.2 = (f32[1024,1]{0,1:T(1,128)S(1)}, f32[1024,1]{0,1:T(1,128)S(1)}, u32[]{:S(2)}, u32[]{:S(2)}) collective-permute-start(f32[1024,1]{0,1:T(1,128)S(1)} %get-tuple-element.50), channel_id=1, source_target_pairs={{0,1},{1,2},{2,3},{3,4},{4,5},{5,6},{6,7},{7,8},{8,9},{9,10},{10,1... | collective-permute-start | bytes 12296 | tf_op jit(solution)/shard_map/ppermute | solution.py:19
  78.9 35.4 %collective-permute-start.3 = (f32[1024,1]{0,1:T(1,128)S(1)}, f32[1024,1]{0,1:T(1,128)S(1)}, u32[]{:S(2)}, u32[]{:S(2)}) collective-permute-start(f32[1024,1]{0,1:T(1,128)S(1)} %get-tuple-element.51), channel_id=1, source_target_pairs={{1,0},{2,1},{3,2},{4,3},{5,4},{6,5},{7,6},{8,7},{9,8},{10,9},{11,1... | collective-permute-start | bytes 12296 | tf_op jit(solution)/shard_map/ppermute | solution.py:21
  114.5 1.0 copy-start.10
  115.5 1.0 copy-start.6
  116.7 1.2 copy-start.3
  118.6 34.1 %collective-permute-start.4 = (f32[1024,1]{0,1:T(1,128)S(1)}, f32[1024,1]{0,1:T(1,128)S(1)}, u32[]{:S(2)}, u32[]{:S(2)}) collective-permute-start(f32[1024,1]{0,1:T(1,128)S(1)} %get-tuple-element.48), channel_id=1, source_target_pairs={{0,1},{1,2},{2,3},{3,4},{4,5},{5,6},{6,7},{7,8},{8,9},{9,10},{10,1... | collective-permute-start | bytes 12296 | tf_op jit(solution)/shard_map/ppermute | solution.py:19
  118.6 36.0 %collective-permute-start.5 = (f32[1024,1]{0,1:T(1,128)}, f32[1024,1]{0,1:T(1,128)}, u32[]{:S(2)}, u32[]{:S(2)}) collective-permute-start(f32[1024,1]{0,1:T(1,128)} %get-tuple-element.49), channel_id=1, source_target_pairs={{1,0},{2,1},{3,2},{4,3},{5,4},{6,5},{7,6},{8,7},{9,8},{10,9},{11,1... | collective-permute-start | bytes 12296 | tf_op jit(solution)/shard_map/ppermute | solution.py:21
  152.6 0.6 copy-start.22
  154.5 1.5 copy-start.16
  155.2 0.7 copy-start.21
  155.4 1.0 copy-start.11
  157.7 0.9 copy-start.12
  158.6 3.9 %copy-start.4 = (f32[512,256]{0,1:T(8,128)S(1)}, f32[512,256]{0,1:T(8,128)}, u32[]{:S(2)}) copy-start(f32[512,256]{0,1:T(8,128)} %copy-done.3) | copy-start | bytes 1572868
  161.1 1.4 copy-start.13
  161.1 1.4 copy-start.17
  165.1 0.8 copy-start.18
  165.1 35.4 %copy-start.15 = (f32[512,256]{0,1:T(8,128)}, f32[512,256]{0,1:T(8,128)S(1)}, u32[]{:S(2)}) copy-start(f32[512,256]{0,1:T(8,128)S(1)} %get-tuple-element.35) | copy-start | bytes 1572868
  166.5 36.5 %collective-permute-start.7 = (f32[1024,1]{0,1:T(1,128)}, f32[1024,1]{0,1:T(1,128)}, u32[]{:S(2)}, u32[]{:S(2)}) collective-permute-start(f32[1024,1]{0,1:T(1,128)} %get-tuple-element.46), channel_id=1, source_target_pairs={{1,0},{2,1},{3,2},{4,3},{5,4},{6,5},{7,6},{8,7},{9,8},{10,9},{11,1... | collective-permute-start | bytes 12296 | tf_op jit(solution)/shard_map/ppermute | solution.py:21
  166.5 34.0 %collective-permute-start.6 = (f32[1024,1]{0,1:T(1,128)S(1)}, f32[1024,1]{0,1:T(1,128)S(1)}, u32[]{:S(2)}, u32[]{:S(2)}) collective-permute-start(f32[1024,1]{0,1:T(1,128)S(1)} %get-tuple-element.47), channel_id=1, source_target_pairs={{0,1},{1,2},{2,3},{3,4},{4,5},{5,6},{6,7},{7,8},{8,9},{9,10},{10,1... | collective-permute-start | bytes 12296 | tf_op jit(solution)/shard_map/ppermute | solution.py:19
  202.0 1.8 copy-start.14
  202.0 1.8 copy-start.19
where the time goes:
time: 241 us; the launch traced here: 240 us
  blocking collectives  152 us (63%)
  starting transfers between devices  24.9 us (10%)
  waiting for transfers between devices  21.9 us (9%)
  local copies, waits for them, and re-layouts  13.9 us (6%)
  matrix products  11.5 us (5%)
  other arithmetic  11.2 us (5%)
  between operations  3.84 us (2%)
    psum x4, blocking collectives, local(): lax.psum((pick_column(passed_quantity, is_last), pick_column(own_sum, is_...  122 us
    psum x1, blocking collectives, local(): primal_total, dual_total = lax.psum((primal_part, dual_part), 'section')  30.2 us
    ppermute x4, starting transfers between devices, padded(): lax.ppermute(head, axis, [((i + 1) % count, i) for i in range(count)])  13.2 us
    all_to_all x1, waiting for transfers between devices, local(): lax.all_to_all(state_parts, 'section', split_axis=1, concat_axis=0, tiled...  12.7 us
    unnamed x49, local copies, waits for them, and re-layouts  9.97 us
    all_to_all x1, waiting for transfers between devices, local(): lax.all_to_all(input_parts, 'section', split_axis=1, concat_axis=0, tiled...  9.15 us
    all_to_all x1, starting transfers between devices, local(): lax.all_to_all(input_parts, 'section', split_axis=1, concat_axis=0, tiled...  7.41 us
  transfers between devices with their start and end apart: 10, of which 2 were waited for; matrix products, arithmetic and copies ran while one was open for 3% of the time, Pallas kernels for 0%

commit v1 on v0

v1 whole, which is shorter than its diff:
```python
import functools

import jax
import jax.numpy as jnp
from jax import lax
from jax.experimental import pallas as pl
from jax.experimental.pallas import tpu as pltpu
from jax.sharding import PartitionSpec as P

ITERS = 4
RHO = 1.0
LANES = 128
CHUNK = 512
ROWS = 64
NT = (((1,), (1,)), ((), ()))


def dot(a, b):
    return jnp.dot(a, b, preferred_element_type=jnp.float32)


def partner(me, k, n, sign):
    if n & (n - 1):
        return lax.rem(me + sign * k + n, n)
    other = me
    for bit in range(n.bit_length()):
        if (k >> bit) & 1:
            other = other + (1 - 2 * ((me // (1 << bit)) % 2)) * (1 << bit)
    return other


def kernel(
    n, width,
    a_hbm, b_hbm, k_hbm, cs_hbm, ci_hbm, start_ref, period_ref,
    x_out, u_out, z_out, norm_out,
    ab, gt, kkt, cs, ci, recv_s, recv_i, cpad, hsend, recv_h, hcol,
    negc, rhs, w, wb, pred, y, v, z, g, xo, uo, zo, part, recv_p,
    load_sem, own_sem, send_sem, recv_sem, out_sem,
):
    me = lax.axis_index("section")
    nx = a_hbm.shape[0]
    nu = b_hbm.shape[1]
    rs, ri = cs.shape[0], ci.shape[0]
    ext = width + LANES
    start = start_ref[0]
    period = period_ref[0]

    def cols(i):
        return pl.ds(pl.multiple_of(i * width, LANES), width)

    loads = [
        pltpu.make_async_copy(cs_hbm, cs, load_sem.at[0]),
        pltpu.make_async_copy(ci_hbm, ci, load_sem.at[1]),
        pltpu.make_async_copy(cs_hbm.at[:, cols(me)], recv_s.at[me], load_sem.at[2]),
        pltpu.make_async_copy(ci_hbm.at[:, cols(me)], recv_i.at[me], load_sem.at[3]),
        pltpu.make_async_copy(a_hbm, ab.at[:, pl.ds(0, nx)], load_sem.at[4]),
        pltpu.make_async_copy(b_hbm, ab.at[:, pl.ds(nx, nu)], load_sem.at[5]),
        pltpu.make_async_copy(k_hbm, kkt, load_sem.at[6]),
    ]
    for c in loads:
        c.start()

    barrier = pltpu.get_barrier_semaphore()
    for k in range(1, n):
        pl.semaphore_signal(barrier, inc=1, device_id={"section": partner(me, k, n, 1)})
    pl.semaphore_wait(barrier, n - 1)

    loads[0].wait()
    loads[1].wait()

    def copies(kind, k, incoming=False):
        to = partner(me, k, n, 1)
        if kind == 0:
            src, dst = cs.at[:, cols(to)], recv_s
        elif kind == 1:
            src, dst = ci.at[:, cols(to)], recv_i
        elif kind == 2:
            src, dst = hsend.at[to], recv_h
        else:
            src, dst = part, recv_p
        slot = partner(me, k, n, -1) if incoming else me
        return pltpu.make_async_remote_copy(
            src_ref=src, dst_ref=dst.at[slot], send_sem=send_sem.at[kind, k],
            recv_sem=recv_sem.at[kind, slot], device_id={"section": to},
        )

    order = range(n - 1, 0, -1)
    for k in order:
        copies(0, k).start()
        copies(1, k).start()

    row = lax.broadcasted_iota(jnp.int32, (n * 8, 1), 0)
    block = row // 8 - start
    block = jnp.where(block < 0, block + n, block)
    item = row % 8
    end = jnp.minimum(period - block * width, width)
    ahead = block * width + end + item
    ahead = jnp.where(ahead >= period, ahead - period, ahead)
    behind = block * width + item - 8
    behind = jnp.where(behind < 0, behind + period, behind)
    place = jnp.where(item < ITERS, ahead, behind) + start * width
    place = jnp.where(place >= n * width, place - n * width, place)

    cpad[...] = jnp.zeros_like(cpad)

    def pick(j, total):
        at = pl.ds(pl.multiple_of(j * CHUNK, CHUNK), CHUNK)
        cpad[pl.ds(0, rs), :] = cs[:, at]
        cpad[pl.ds(rs, ri), :] = ci[:, at]
        column = lax.broadcasted_iota(jnp.int32, (n * 8, CHUNK), 1) + j * CHUNK
        onehot = jnp.where(column == place, 1.0, 0.0).astype(jnp.bfloat16)
        rest = cpad[...]
        for _ in range(3):
            piece = rest.astype(jnp.bfloat16)
            rest = rest - piece.astype(jnp.float32)
            total = total + lax.dot_general(onehot, piece, NT, preferred_element_type=jnp.float32)
        return total

    picked = lax.fori_loop(
        0, cs.shape[1] // CHUNK, pick, jnp.zeros((n * 8, LANES), jnp.float32)
    )
    hsend[...] = picked.reshape(n, 8, LANES)
    own_halo = pltpu.make_async_copy(hsend.at[me], recv_h.at[me], own_sem.at[0])
    own_halo.start()
    for k in order:
        copies(2, k).start()

    loads[4].wait()
    loads[5].wait()
    loads[6].wait()
    gt[...] = ab[...].T

    loads[2].wait()
    loads[3].wait()
    own_halo.wait()
    for kind in (0, 1, 2):
        for k in order:
            copies(kind, k, True).wait_recv()

    flipped = recv_h[...].reshape(n * 8, LANES).T
    for s in range(n):
        tile = s * 8 // LANES * LANES
        piece = flipped[:, tile:tile + LANES]
        if s * 8 - tile:
            piece = pltpu.roll(piece, LANES - (s * 8 - tile), 1)
        hcol[pl.ds(s * rs, rs), :] = piece[:rs]
        hcol[pl.ds(nx + s * ri, ri), :] = piece[rs:rs + ri]

    mine = me - start
    mine = jnp.where(mine < 0, mine + n, mine)
    finish = jnp.minimum(period - mine * width, width)
    lane = lax.broadcasted_iota(jnp.int32, (1, LANES), 1)

    for s in range(n):
        negc[pl.ds(s * rs, rs), pl.ds(0, width)] = -recv_s[s]
        negc[pl.ds(nx + s * ri, ri), pl.ds(0, width)] = -recv_i[s]
    for r in range(0, nx + nu, ROWS):
        at = pl.ds(r, ROWS)
        h = -hcol[at, :]
        back = pltpu.roll(h, LANES - 8, 1)
        fills = [jnp.broadcast_to(h[:, i:i + 1], (ROWS, LANES)) for i in range(ITERS)]
        for t in range(0, ext, LANES):
            if t < width:
                value = negc[at, pl.ds(t, LANES)]
            else:
                value = jnp.where(lane >= LANES - ITERS, back, 0.0)
            for i in range(ITERS):
                value = jnp.where(lane + t == finish + i, fills[i], value)
            negc[at, pl.ds(t, LANES)] = value
            rhs[at, pl.ds(t, LANES)] = value.astype(jnp.bfloat16)

    ids = mine * width + lax.broadcasted_iota(jnp.int32, (1, width), 1)
    active = ids < period
    primal = jnp.zeros((8, LANES), jnp.float32)
    dual = jnp.zeros((8, LANES), jnp.float32)

    def fold(value):
        total = jnp.zeros((8, LANES), jnp.float32)
        for a in range(0, value.shape[0], 8):
            for b in range(0, value.shape[1], LANES):
                total = total + value[a:a + 8, b:b + LANES]
        return total

    for it in range(ITERS):
        last = it == ITERS - 1
        if it > 0:
            w[...] = dot(gt[...], g[...])
            for r in range(0, nx + nu, ROWS):
                at = pl.ds(r, ROWS)
                if r < nx:
                    value = negc[at, :] + RHO * (z[at, :] - y[at, :]) + RHO * w[at, :]
                else:
                    value = negc[at, :] + RHO * w[at, :]
                rhs[at, :] = value.astype(jnp.bfloat16)
        w[...] = dot(kkt[...], rhs[...])
        for r in range(0, nx + nu, ROWS):
            at = pl.ds(r, ROWS)
            wb[at, :] = w[at, :].astype(jnp.bfloat16)
        pred[...] = dot(ab[...], wb[...])
        for r in range(0, nx, ROWS):
            at = pl.ds(r, ROWS)
            x = w[at, :]
            q = pred[at, :]
            own = x + y[at, :] if it else x
            link = q + v[at, :] if it else q
            znew = 0.5 * (own + pltpu.roll(link, 1, 1))
            znext = pltpu.roll(znew, ext - 1, 1)
            if not last:
                y[at, :] = own - znew
                vnew = link - znext
                v[at, :] = vnew
                g[at, :] = (znext - vnew).astype(jnp.bfloat16)
                z[at, :] = znew
            else:
                miss = (x - znew) ** 2 + (q - znext) ** 2
                primal = primal + fold(jnp.where(active, miss[:, :width], 0.0))
                change = znew - z[at, :] if it else znew
                dual = dual + fold(jnp.where(active, (change * change)[:, :width], 0.0))
                xo[at, :] = jnp.where(active, x[:, :width], 0.0)
                zo[at, :] = jnp.where(active, znew[:, :width], 0.0)
    part[pl.ds(0, 8), :] = primal
    part[pl.ds(8, 8), :] = RHO * RHO * dual
    recv_p[me] = part[...]
    for k in order:
        copies(3, k).start()
    for r in range(0, nu, ROWS):
        uo[pl.ds(r, ROWS), :] = jnp.where(active, w[pl.ds(nx + r, ROWS), pl.ds(0, width)], 0.0)
    outs = [
        pltpu.make_async_copy(xo, x_out, out_sem.at[0]),
        pltpu.make_async_copy(uo, u_out, out_sem.at[1]),
        pltpu.make_async_copy(zo, z_out, out_sem.at[2]),
    ]
    for c in outs:
        c.start()
    for k in order:
        copies(3, k, True).wait_recv()
    total = recv_p[0]
    for s in range(1, n):
        total = total + recv_p[s]
    top = jnp.sqrt(jnp.broadcast_to(jnp.sum(total[:8], keepdims=True), (8, LANES)))
    low = jnp.sqrt(jnp.broadcast_to(jnp.sum(total[8:], keepdims=True), (8, LANES)))
    norm_out[0] = jnp.max(top)
    norm_out[1] = jnp.max(low)
    for c in outs:
        c.wait()
    for kind in (0, 1, 2, 3):
        for k in order:
            copies(kind, k).wait_send()


def local(a, b, kkt, lin_state, lin_input, block_start, period):
    n = lax.axis_size("section")
    width = lin_state.shape[1] // n
    ext = width + LANES
    nx, nu = b.shape
    nw = nx + nu
    rs, ri = lin_state.shape[0], lin_input.shape[0]
    f32, bf16 = jnp.float32, jnp.bfloat16
    anyspec = pl.BlockSpec(memory_space=pl.ANY)
    smem = pl.BlockSpec(memory_space=pltpu.SMEM)
    vmem = pltpu.VMEM
    return pl.pallas_call(
        functools.partial(kernel, n, width),
        name="admm",
        out_shape=(
            jax.ShapeDtypeStruct((nx, width), f32),
            jax.ShapeDtypeStruct((nu, width), f32),
            jax.ShapeDtypeStruct((nx, width), f32),
            jax.ShapeDtypeStruct((2,), f32),
        ),
        in_specs=[anyspec] * 5 + [smem] * 2,
        out_specs=(anyspec, anyspec, anyspec, smem),
        scratch_shapes=[
            vmem((nx, nw), bf16), vmem((nw, nx), bf16), vmem((nw, nw), bf16),
            vmem(lin_state.shape, f32), vmem(lin_input.shape, f32),
            vmem((n, rs, width), f32), vmem((n, ri, width), f32),
            vmem((LANES, CHUNK), f32),
            vmem((n, 8, LANES), f32), vmem((n, 8, LANES), f32), vmem((nw, LANES), f32),
            vmem((nw, ext), f32), vmem((nw, ext), bf16), vmem((nw, ext), f32),
            vmem((nw, ext), bf16), vmem((nx, ext), f32),
            vmem((nx, ext), f32), vmem((nx, ext), f32), vmem((nx, ext), f32),
            vmem((nx, ext), bf16),
            vmem((nx, width), f32), vmem((nu, width), f32), vmem((nx, width), f32),
            vmem((16, LANES), f32), vmem((n, 16, LANES), f32),
            pltpu.SemaphoreType.DMA((7,)), pltpu.SemaphoreType.DMA((1,)),
            pltpu.SemaphoreType.DMA((4, n)), pltpu.SemaphoreType.DMA((4, n)),
            pltpu.SemaphoreType.DMA((3,)),
        ],
        compiler_params=pltpu.CompilerParams(
            collective_id=0, has_side_effects=True, vmem_limit_bytes=48 * 1024 * 1024
        ),
    )(a, b, kkt, lin_state, lin_input, block_start, period)


def solution(mesh):
    return jax.shard_map(
        local,
        mesh=mesh,
        in_specs=(
            P("plant", None),
            P("plant", None),
            P("plant", None),
            P(("plant", "section"), None),
            P(("plant", "section"), None),
            P("plant"),
            P("plant"),
        ),
        out_specs=(P("plant", "section"), P("plant", "section"), P("plant", "section"), P("plant")),
        check_vma=False,
    )
```

time: 241 us -> 52.3 us (0.22)
  blocking collectives: 152 us -> 0 us
  Pallas kernels: 0 us -> 42 us
  starting transfers between devices: 24.9 us -> 0 us
  waiting for transfers between devices: 21.9 us -> 0 us
  matrix products: 11.5 us -> 0 us
  other arithmetic: 11.2 us -> 0 us
  local copies, waits for them, and re-layouts: 13.9 us -> 8.05 us
    psum x5 -> x0, blocking collectives: 152 us -> none  [the longest x4 122 us: local(): lax.psum((pick_column(passed_quantity, is_last), pick_column(own_sum, is_...]
    pallas_call x0 -> x1, Pallas kernels: none -> 42 us  [local(): pl.pallas_call(functools.partial(kernel, n, width), name='admm', out_shap...]
    all_to_all x2 -> x0, waiting for transfers between devices: 21.9 us -> none  [the longest x1 12.7 us: local(): lax.all_to_all(state_parts, 'section', split_axis=1, concat_axis=0, tiled...]
    ppermute x8 -> x0, starting transfers between devices: 13.9 us -> none  [the longest x4 13.2 us: padded(): lax.ppermute(head, axis, [((i + 1) % count, i) for i in range(count)])]
    dot_general x18 -> x0, matrix products: 11.5 us -> none  [the longest x4 4.7 us: estimate_condition(): jnp.dot(control_gain_array, rounded[condition_lines:], preferred_element_...]
    all_to_all x2 -> x0, starting transfers between devices: 11 us -> none  [the longest x1 7.41 us: local(): lax.all_to_all(input_parts, 'section', split_axis=1, concat_axis=0, tiled...]
    sub x3 -> x0, other arithmetic: 3.77 us -> none  [local(): consensus - dual_state]
    reshape x2 -> x0, local copies, waits for them, and re-layouts: 2.65 us -> none  [the longest x1 1.8 us: local(): input_parts = lin_input.reshape(lin_input.shape[0], cycle_size, block_width)]
  transfers between devices with their start and end apart: 10 -> 0, of which waited for: 2 -> 0; matrix products, arithmetic and copies ran while one was open for 3% -> 0% of each run, Pallas kernels for 0% -> 0%
where the time goes in v1:
time: 52.3 us; the launch traced here: 52 us
  Pallas kernels  42 us (80%)
  local copies, waits for them, and re-layouts  8.05 us (15%)
  between operations  1.95 us (4%)
    pallas_call x1, Pallas kernels, local(): pl.pallas_call(functools.partial(kernel, n, width), name='admm', out_shap...  42 us
    unnamed x14, local copies, waits for them, and re-layouts  8.05 us

profile of v1, /device:TPU:0, one launch (start us, length us, event | category | flops | bytes accessed | tf_op | source)
XLA Modules:
  0.0 52.0 jit_solution(3485131961139606608)
XLA Ops:
  1.9 0.0 copy-start
  1.9 1.3 %copy-done = bf16[768,768]{1,0:T(8,128)(2,1)S(1)} copy-done((bf16[768,768]{1,0:T(8,128)(2,1)S(1)}, bf16[768,768]{1,0:T(8,128)(2,1)}, u32[]{:S(2)}) %copy-start) | copy-done | bytes 1179672
  3.2 0.0 copy-start.1
  3.2 1.0 %copy-done.1 = bf16[512,512]{1,0:T(8,128)(2,1)S(1)} copy-done((bf16[512,512]{1,0:T(8,128)(2,1)S(1)}, bf16[512,512]{1,0:T(8,128)(2,1)}, u32[]{:S(2)}) %copy-start.1) | copy-done | bytes 524312
  4.2 0.0 copy-start.2
  4.2 1.0 %copy-done.2 = f32[32,4096]{1,0:T(8,128)S(1)} copy-done((f32[32,4096]{1,0:T(8,128)S(1)}, f32[32,4096]{1,0:T(8,128)}, u32[]{:S(2)}) %copy-start.2) | copy-done | bytes 524312
  5.3 0.0 copy-start.3
  5.3 0.9 %copy-done.3 = bf16[512,256]{1,0:T(8,128)(2,1)S(1)} copy-done((bf16[512,256]{1,0:T(8,128)(2,1)S(1)}, bf16[512,256]{1,0:T(8,128)(2,1)}, u32[]{:S(2)}) %copy-start.3) | copy-done | bytes 262168
  6.2 0.0 copy-start.4
  6.2 0.9 %copy-done.4 = f32[16,4096]{1,0:T(8,128)S(1)} copy-done((f32[16,4096]{1,0:T(8,128)S(1)}, f32[16,4096]{1,0:T(8,128)}, u32[]{:S(2)}) %copy-start.4) | copy-done | bytes 262168
  7.2 42.0 %admm.1 = (f32[512,256]{1,0:T(8,128)S(1)}, f32[256,256]{1,0:T(8,128)S(1)}, f32[512,256]{1,0:T(8,128)S(1)}, f32[2]{0:T(128)S(1)}) custom-call(bf16[512,512]{1,0:T(8,128)(2,1)S(1)} %copy-done.1, bf16[512,256]{1,0:T(8,128)(2,1)S(1)} %copy-done.3, bf16[768,768]{1,0:T(8,128)(2,1)S(1)} %copy-done, f32[32,4096]{1,0:T(8,128)S(1)} %copy-done.2, ...), custom_call_target="tpu_custom_call" | custom-call | tf_op jit(solution)/shard_map/admm/pallas_call | solution.py:262
  49.2 0.8 %copy.17 = f32[512,256]{1,0:T(8,128)} copy(f32[512,256]{1,0:T(8,128)S(1)} %get-tuple-element.8) | data formatting | bytes 1048576
  50.0 0.7 %copy.18 = f32[256,256]{1,0:T(8,128)} copy(f32[256,256]{1,0:T(8,128)S(1)} %get-tuple-element.9) | data formatting | bytes 524288
  50.7 0.8 %copy.19 = f32[512,256]{1,0:T(8,128)} copy(f32[512,256]{1,0:T(8,128)S(1)} %get-tuple-element.10) | data formatting | bytes 1048576
  51.5 0.5 copy.20
Async XLA Ops:
  1.9 1.3 %copy-start = (bf16[768,768]{1,0:T(8,128)(2,1)S(1)}, bf16[768,768]{1,0:T(8,128)(2,1)}, u32[]{:S(2)}) copy-start(bf16[768,768]{1,0:T(8,128)(2,1)} %k_hbm.1) | copy-start | bytes 3538948
  3.2 1.0 %copy-start.1 = (bf16[512,512]{1,0:T(8,128)(2,1)S(1)}, bf16[512,512]{1,0:T(8,128)(2,1)}, u32[]{:S(2)}) copy-start(bf16[512,512]{1,0:T(8,128)(2,1)} %a_hbm.1) | copy-start | bytes 1572868
  4.2 1.0 %copy-start.2 = (f32[32,4096]{1,0:T(8,128)S(1)}, f32[32,4096]{1,0:T(8,128)}, u32[]{:S(2)}) copy-start(f32[32,4096]{1,0:T(8,128)} %cs_hbm.1) | copy-start | bytes 1572868
  5.3 0.9 %copy-start.3 = (bf16[512,256]{1,0:T(8,128)(2,1)S(1)}, bf16[512,256]{1,0:T(8,128)(2,1)}, u32[]{:S(2)}) copy-start(bf16[512,256]{1,0:T(8,128)(2,1)} %b_hbm.1) | copy-start | bytes 786436
  6.2 0.9 %copy-start.4 = (f32[16,4096]{1,0:T(8,128)S(1)}, f32[16,4096]{1,0:T(8,128)}, u32[]{:S(2)}) copy-start(f32[16,4096]{1,0:T(8,128)} %ci_hbm.1) | copy-start | bytes 786436

commit v2 on v1

v2 whole, which is shorter than its diff:
```python
import functools

import jax
import jax.numpy as jnp
from jax import lax
from jax.experimental import pallas as pl
from jax.experimental.pallas import tpu as pltpu
from jax.sharding import PartitionSpec as P

ITERS = 4
RHO = 1.0
LANES = 128
CHUNK = 512
ROWS = 64
PARTS = 2
NT = (((1,), (1,)), ((), ()))


def dot(a, b):
    return jnp.dot(a, b, preferred_element_type=jnp.float32)


def partner(me, k, n, sign):
    if n & (n - 1):
        return lax.rem(me + sign * k + n, n)
    other = me
    for bit in range(n.bit_length()):
        if (k >> bit) & 1:
            other = other + (1 - 2 * ((me // (1 << bit)) % 2)) * (1 << bit)
    return other


def kernel(
    n, width,
    a_hbm, b_hbm, k_hbm, cs_hbm, ci_hbm, start_ref, period_ref,
    x_out, u_out, z_out, norm_out,
    ab, gt, kkt, cs, ci, recv_s, recv_i, cpad, hsend, recv_h, hcol,
    negc, rhs, w, wb, pred, y, v, z, g, xo, uo, zo, part, recv_p,
    load_sem, own_sem, send_sem, recv_sem, out_sem,
):
    me = lax.axis_index("section")
    nx = a_hbm.shape[0]
    nu = b_hbm.shape[1]
    rs, ri = cs.shape[0], ci.shape[0]
    pw = width // PARTS
    ext = pw + LANES
    shift = LANES // PARTS
    start = start_ref[0]
    period = period_ref[0]

    def cols(i, h):
        return pl.ds(pl.multiple_of(i * width + h * pw, LANES), pw)

    loads = [
        pltpu.make_async_copy(cs_hbm, cs, load_sem.at[0]),
        pltpu.make_async_copy(ci_hbm, ci, load_sem.at[1]),
        pltpu.make_async_copy(a_hbm, ab.at[:, pl.ds(0, nx)], load_sem.at[2]),
        pltpu.make_async_copy(b_hbm, ab.at[:, pl.ds(nx, nu)], load_sem.at[3]),
        pltpu.make_async_copy(k_hbm, kkt, load_sem.at[4]),
    ]
    for h in range(PARTS):
        loads += [
            pltpu.make_async_copy(
                cs_hbm.at[:, cols(me, h)], recv_s.at[h, me], load_sem.at[5 + 2 * h]
            ),
            pltpu.make_async_copy(
                ci_hbm.at[:, cols(me, h)], recv_i.at[h, me], load_sem.at[6 + 2 * h]
            ),
        ]
    for c in loads:
        c.start()

    barrier = pltpu.get_barrier_semaphore()
    for k in range(1, n):
        pl.semaphore_signal(barrier, inc=1, device_id={"section": partner(me, k, n, 1)})
    pl.semaphore_wait(barrier, n - 1)

    loads[0].wait()
    loads[1].wait()

    def copies(kind, k, incoming=False):
        to = partner(me, k, n, 1)
        if kind == 0:
            src, dst = part, recv_p
        elif kind == 1:
            src, dst = hsend.at[to], recv_h
        elif kind % 2 == 0:
            src, dst = cs.at[:, cols(to, kind // 2 - 1)], recv_s.at[kind // 2 - 1]
        else:
            src, dst = ci.at[:, cols(to, kind // 2 - 1)], recv_i.at[kind // 2 - 1]
        slot = partner(me, k, n, -1) if incoming else me
        return pltpu.make_async_remote_copy(
            src_ref=src, dst_ref=dst.at[slot], send_sem=send_sem.at[kind, k],
            recv_sem=recv_sem.at[kind, slot], device_id={"section": to},
        )

    order = list(range(1, n // 2)) + list(range(n - 1, n // 2 - 1, -1))
    for k in order:
        copies(2, k).start()
        copies(3, k).start()

    row = lax.broadcasted_iota(jnp.int32, (n * PARTS * 8, 1), 0)
    block = row // (PARTS * 8) - start
    block = jnp.where(block < 0, block + n, block)
    base = block * width + (row // 8) % PARTS * pw
    item = row % 8
    end = jnp.minimum(period - base, pw)
    ahead = base + end + item
    ahead = jnp.where(ahead >= period, ahead - period, ahead)
    behind = base + item - 8
    behind = jnp.where(behind < 0, behind + period, behind)
    place = jnp.where(item < ITERS, ahead, behind) + start * width
    place = jnp.where(place >= n * width, place - n * width, place)

    cpad[...] = jnp.zeros_like(cpad)

    def pick(j, total):
        at = pl.ds(pl.multiple_of(j * CHUNK, CHUNK), CHUNK)
        cpad[pl.ds(0, rs), :] = cs[:, at]
        cpad[pl.ds(rs, ri), :] = ci[:, at]
        column = lax.broadcasted_iota(jnp.int32, (n * PARTS * 8, CHUNK), 1) + j * CHUNK
        onehot = jnp.where(column == place, 1.0, 0.0).astype(jnp.bfloat16)
        rest = cpad[...]
        for _ in range(3):
            piece = rest.astype(jnp.bfloat16)
            rest = rest - piece.astype(jnp.float32)
            total = total + lax.dot_general(onehot, piece, NT, preferred_element_type=jnp.float32)
        return total

    picked = lax.fori_loop(
        0, cs.shape[1] // CHUNK, pick, jnp.zeros((n * PARTS * 8, LANES), jnp.float32)
    )
    picked = picked.reshape(n, PARTS, 8, LANES)
    packed = picked[:, 0].reshape(n * 8, LANES)
    for h in range(1, PARTS):
        packed = packed + pltpu.roll(picked[:, h].reshape(n * 8, LANES), h * shift, 1)
    hsend[...] = packed.reshape(n, 8, LANES)
    own_halo = pltpu.make_async_copy(hsend.at[me], recv_h.at[me], own_sem.at[0])
    own_halo.start()
    for k in order:
        copies(1, k).start()
    for h in range(1, PARTS):
        for k in order:
            copies(2 + 2 * h, k).start()
            copies(3 + 2 * h, k).start()

    loads[2].wait()
    loads[3].wait()
    loads[4].wait()
    gt[...] = ab[...].T

    own_halo.wait()
    for k in order:
        copies(1, k, True).wait_recv()

    flipped = recv_h[...].reshape(n * 8, LANES).T
    for s in range(n):
        tile = s * 8 // LANES * LANES
        piece = flipped[:, tile:tile + LANES]
        if s * 8 - tile:
            piece = pltpu.roll(piece, LANES - (s * 8 - tile), 1)
        for h in range(PARTS):
            top = h * shift
            hcol[h, pl.ds(s * rs, rs), :] = piece[top:top + rs]
            hcol[h, pl.ds(nx + s * ri, ri), :] = piece[top + rs:top + rs + ri]

    mine = me - start
    mine = jnp.where(mine < 0, mine + n, mine)
    lane = lax.broadcasted_iota(jnp.int32, (1, LANES), 1)
    primal = jnp.zeros((8, LANES), jnp.float32)
    dual = jnp.zeros((8, LANES), jnp.float32)

    def fold(value):
        total = jnp.zeros((8, LANES), jnp.float32)
        for a in range(0, value.shape[0], 8):
            for b in range(0, value.shape[1], LANES):
                total = total + value[a:a + 8, b:b + LANES]
        return total

    for h in range(PARTS):
        base = mine * width + h * pw
        finish = jnp.minimum(period - base, pw)
        own_cols = pl.ds(h * pw, pw)
        loads[5 + 2 * h].wait()
        loads[6 + 2 * h].wait()
        for k in order:
            copies(2 + 2 * h, k, True).wait_recv()
            copies(3 + 2 * h, k, True).wait_recv()

        for s in range(n):
            negc[pl.ds(s * rs, rs), pl.ds(0, pw)] = -recv_s[h, s]
            negc[pl.ds(nx + s * ri, ri), pl.ds(0, pw)] = -recv_i[h, s]
        for r in range(0, nx + nu, ROWS):
            at = pl.ds(r, ROWS)
            halo = -hcol[h, at, :]
            back = pltpu.roll(halo, LANES - 8, 1)
            fills = [jnp.broadcast_to(halo[:, i:i + 1], (ROWS, LANES)) for i in range(ITERS)]
            for t in range(0, ext, LANES):
                if t < pw:
                    value = negc[at, pl.ds(t, LANES)]
                else:
                    value = jnp.where(lane >= LANES - ITERS, back, 0.0)
                for i in range(ITERS):
                    value = jnp.where(lane + t == finish + i, fills[i], value)
                negc[at, pl.ds(t, LANES)] = value
                rhs[at, pl.ds(t, LANES)] = value.astype(jnp.bfloat16)

        ids = base + lax.broadcasted_iota(jnp.int32, (1, pw), 1)
        active = ids < period
        for it in range(ITERS):
            last = it == ITERS - 1
            if it > 0:
                w[...] = dot(gt[...], g[...])
                for r in range(0, nx + nu, ROWS):
                    at = pl.ds(r, ROWS)
                    if r < nx:
                        value = negc[at, :] + RHO * (z[at, :] - y[at, :]) + RHO * w[at, :]
                    else:
                        value = negc[at, :] + RHO * w[at, :]
                    rhs[at, :] = value.astype(jnp.bfloat16)
            w[...] = dot(kkt[...], rhs[...])
            for r in range(0, nx + nu, ROWS):
                at = pl.ds(r, ROWS)
                wb[at, :] = w[at, :].astype(jnp.bfloat16)
            pred[...] = dot(ab[...], wb[...])
            for r in range(0, nx, ROWS):
                at = pl.ds(r, ROWS)
                x = w[at, :]
                q = pred[at, :]
                own = x + y[at, :] if it else x
                link = q + v[at, :] if it else q
                znew = 0.5 * (own + pltpu.roll(link, 1, 1))
                znext = pltpu.roll(znew, ext - 1, 1)
                if not last:
                    y[at, :] = own - znew
                    vnew = link - znext
                    v[at, :] = vnew
                    g[at, :] = (znext - vnew).astype(jnp.bfloat16)
                    z[at, :] = znew
                else:
                    miss = (x - znew) ** 2 + (q - znext) ** 2
                    primal = primal + fold(jnp.where(active, miss[:, :pw], 0.0))
                    change = znew - z[at, :] if it else znew
                    dual = dual + fold(jnp.where(active, (change * change)[:, :pw], 0.0))
                    xo[at, own_cols] = jnp.where(active, x[:, :pw], 0.0)
                    zo[at, own_cols] = jnp.where(active, znew[:, :pw], 0.0)
        for r in range(0, nu, ROWS):
            uo[pl.ds(r, ROWS), own_cols] = jnp.where(
                active, w[pl.ds(nx + r, ROWS), pl.ds(0, pw)], 0.0
            )
    part[pl.ds(0, 8), :] = primal
    part[pl.ds(8, 8), :] = RHO * RHO * dual
    recv_p[me] = part[...]
    for k in order:
        copies(0, k).start()
    outs = [
        pltpu.make_async_copy(xo, x_out, out_sem.at[0]),
        pltpu.make_async_copy(uo, u_out, out_sem.at[1]),
        pltpu.make_async_copy(zo, z_out, out_sem.at[2]),
    ]
    for c in outs:
        c.start()
    for k in order:
        copies(0, k, True).wait_recv()
    total = recv_p[0]
    for s in range(1, n):
        total = total + recv_p[s]
    top = jnp.sqrt(jnp.broadcast_to(jnp.sum(total[:8], keepdims=True), (8, LANES)))
    low = jnp.sqrt(jnp.broadcast_to(jnp.sum(total[8:], keepdims=True), (8, LANES)))
    norm_out[0] = jnp.max(top)
    norm_out[1] = jnp.max(low)
    for c in outs:
        c.wait()
    for kind in range(2 + 2 * PARTS):
        for k in order:
            copies(kind, k).wait_send()


def local(a, b, kkt, lin_state, lin_input, block_start, period):
    n = lax.axis_size("section")
    width = lin_state.shape[1] // n
    pw = width // PARTS
    ext = pw + LANES
    nx, nu = b.shape
    nw = nx + nu
    rs, ri = lin_state.shape[0], lin_input.shape[0]
    f32, bf16 = jnp.float32, jnp.bfloat16
    anyspec = pl.BlockSpec(memory_space=pl.ANY)
    smem = pl.BlockSpec(memory_space=pltpu.SMEM)
    vmem = pltpu.VMEM
    return pl.pallas_call(
        functools.partial(kernel, n, width),
        name="admm",
        out_shape=(
            jax.ShapeDtypeStruct((nx, width), f32),
            jax.ShapeDtypeStruct((nu, width), f32),
            jax.ShapeDtypeStruct((nx, width), f32),
            jax.ShapeDtypeStruct((2,), f32),
        ),
        in_specs=[anyspec] * 5 + [smem] * 2,
        out_specs=(anyspec, anyspec, anyspec, smem),
        scratch_shapes=[
            vmem((nx, nw), bf16), vmem((nw, nx), bf16), vmem((nw, nw), bf16),
            vmem(lin_state.shape, f32), vmem(lin_input.shape, f32),
            vmem((PARTS, n, rs, pw), f32), vmem((PARTS, n, ri, pw), f32),
            vmem((LANES, CHUNK), f32),
            vmem((n, 8, LANES), f32), vmem((n, 8, LANES), f32), vmem((PARTS, nw, LANES), f32),
            vmem((nw, ext), f32), vmem((nw, ext), bf16), vmem((nw, ext), f32),
            vmem((nw, ext), bf16), vmem((nx, ext), f32),
            vmem((nx, ext), f32), vmem((nx, ext), f32), vmem((nx, ext), f32),
            vmem((nx, ext), bf16),
            vmem((nx, width), f32), vmem((nu, width), f32), vmem((nx, width), f32),
            vmem((16, LANES), f32), vmem((n, 16, LANES), f32),
            pltpu.SemaphoreType.DMA((5 + 2 * PARTS,)), pltpu.SemaphoreType.DMA((1,)),
            pltpu.SemaphoreType.DMA((2 + 2 * PARTS, n)), pltpu.SemaphoreType.DMA((2 + 2 * PARTS, n)),
            pltpu.SemaphoreType.DMA((3,)),
        ],
        compiler_params=pltpu.CompilerParams(
            collective_id=0, has_side_effects=True, vmem_limit_bytes=62000000
        ),
    )(a, b, kkt, lin_state, lin_input, block_start, period)


def solution(mesh):
    return jax.shard_map(
        local,
        mesh=mesh,
        in_specs=(
            P("plant", None),
            P("plant", None),
            P("plant", None),
            P(("plant", "section"), None),
            P(("plant", "section"), None),
            P("plant"),
            P("plant"),
        ),
        out_specs=(P("plant", "section"), P("plant", "section"), P("plant", "section"), P("plant")),
        check_vma=False,
    )
```

time: 52.3 us -> 47.8 us (0.914)
  local copies, waits for them, and re-layouts: 8.05 us -> 3.96 us
    unnamed x14 -> x10, local copies, waits for them, and re-layouts: 8.05 us -> 3.96 us
where the time goes in v2:
time: 47.8 us; the launch traced here: 47.6 us
  Pallas kernels  41.7 us (87%)
  local copies, waits for them, and re-layouts  3.96 us (8%)
  between operations  1.96 us (4%)
    pallas_call x1, Pallas kernels, local(): pl.pallas_call(functools.partial(kernel, n, width), name='admm', out_shap...  41.7 us
    unnamed x10, local copies, waits for them, and re-layouts  3.96 us

profile of v2, /device:TPU:0, one launch (start us, length us, event | category | flops | bytes accessed | tf_op | source)
XLA Modules:
  0.0 47.6 jit_solution(6376472331389620053)
XLA Ops:
  1.9 41.7 %admm.1 = (f32[512,256]{1,0:T(8,128)}, f32[256,256]{1,0:T(8,128)}, f32[512,256]{1,0:T(8,128)}, f32[2]{0:T(128)}) custom-call(bf16[512,512]{1,0:T(8,128)(2,1)} %a_hbm.1, bf16[512,256]{1,0:T(8,128)(2,1)} %b_hbm.1, bf16[768,768]{1,0:T(8,128)(2,1)} %k_hbm.1, f32[32,4096]{1,0:T(8,128)} %cs_hbm.1, f32[16,4096]{1,0:T(8,128)} %ci_hbm.1, s32[1]{0:T(128)S(6)} %copy.15.start_ref, ...), custom_call_target="tpu_custom_call" | custom-call | tf_op jit(solution)/shard_map/admm/pallas_call | solution.py:291
  43.6 0.0 copy-start.1
  43.7 0.0 copy-start
  43.7 0.0 copy-start.2
  43.7 1.9 %copy.17 = f32[512,256]{1,0:T(8,128)} copy(f32[512,256]{1,0:T(8,128)} %get-tuple-element.8) | data formatting | bytes 1048576
  45.6 0.0 copy-done.1
  45.6 0.7 %copy.18 = f32[256,256]{1,0:T(8,128)} copy(f32[256,256]{1,0:T(8,128)S(1)} %copy-done.1) | data formatting | bytes 524288
  46.3 0.0 copy-done
  46.3 0.8 %copy.19 = f32[512,256]{1,0:T(8,128)} copy(f32[512,256]{1,0:T(8,128)S(1)} %copy-done) | data formatting | bytes 1048576
  47.1 0.0 copy-done.2
  47.1 0.5 %copy.20 = f32[2]{0:T(128)} copy(f32[2]{0:T(128)S(1)} %copy-done.2) | data formatting | bytes 16
Async XLA Ops:
  43.6 2.0 %copy-start.1 = (f32[256,256]{1,0:T(8,128)S(1)}, f32[256,256]{1,0:T(8,128)}, u32[]{:S(2)}) copy-start(f32[256,256]{1,0:T(8,128)} %get-tuple-element.9) | copy-start | bytes 786436
  43.7 2.7 %copy-start = (f32[512,256]{1,0:T(8,128)S(1)}, f32[512,256]{1,0:T(8,128)}, u32[]{:S(2)}) copy-start(f32[512,256]{1,0:T(8,128)} %get-tuple-element.10) | copy-start | bytes 1572868
  43.7 3.5 %copy-start.2 = (f32[2]{0:T(128)S(1)}, f32[2]{0:T(128)}, u32[]{:S(2)}) copy-start(f32[2]{0:T(128)} %get-tuple-element.11) | copy-start | bytes 28
